TPU v7x, 32 devices: a whole 2x2x4 slice. The times are simulated.
32 devices in a mesh: groups: 2 (over x), sph: 16 (over z, y, core).
Axes of the slice: x: 2, y: 2, z: 4, core: 2. Of those that a mesh axis runs over, the one named last changes fastest.
Arguments:
- positions: float32 [512, 3], P('sph'), may hold values from -8 to 8
- wave_vectors: float32 [256, 3], replicated, may hold values from -5 to 5
- pattern: float32 [2, 448, 256], replicated, may hold values from -6 to 6
- dir_index: int32 [64], P('groups'), parts along dimension 0, may hold values from 0 to 255
- mie: float32 [2, 448, 512], P(None, None, 'sph'), may hold values from -0.9 to 0.9
- trans_table: bfloat16 [8, 2, 448, 448], replicated, may hold values from -0.1875 to 0.1875
- pair_route: int32 [1024, 1], P('sph'), may hold values from 0 to 15; in each aligned block of 64 rows (0 to 63, 64 to 127, ...) at most 8 rows name the same one
- pair_source: int32 [1024], P('sph'), may hold values from 0 to 15
- pair_target: int32 [1024], P('sph'), may hold values from 0 to 15
- pair_class: int32 [1024], P('sph'), may hold values from 0 to 7
Outputs:
- scattered: bfloat16 [896, 32768], P(None, ('groups', 'sph')), parts along dimension 1
- extinction: float32 [64], P('groups'), parts along dimension 0
There are 2 independent parts, one for each index of `groups`. A program takes and returns all parts, laid end to end along the dimension named above; an argument that names none is the same for every part. Nothing has to cross between parts.
Inputs may be any that keep to these rules, and one draw needn't show every extreme that they name: `pair_route`: among the rows of one device no device is named by more than 8 pairs, and in every draw some device is named by exactly 8 of them.
All inputs are finite; a program needn't handle non-finite values.
Results may differ from a plain program's by a relative error of at most 0.0051.
Values may be sent and summed in bfloat16 or wider, within the bound.
No kernel may reach another device: no remote copies, remote signals or barrier semaphores. Data moves between devices by JAX's collectives and lax.ppermute only.
A program may use at most 192 MiB of HBM per device.

v0:
```python
import jax
import jax.numpy as jnp
from jax import lax
from jax.sharding import PartitionSpec as P

BLOCK = 2
HIGHEST_PRECISION = lax.Precision.HIGHEST


def incident_field(positions, wave_vectors, pattern, dir_index):
    table_rows = wave_vectors.shape[0]
    select = (jnp.arange(table_rows, dtype=jnp.int32)[:, None] == dir_index[None, :]).astype(
        jnp.float32
    )
    directions = jnp.dot(select.T, wave_vectors, precision=HIGHEST_PRECISION)
    phases = (
        positions[:, 0:1] * directions[None, :, 0]
        + positions[:, 1:2] * directions[None, :, 1]
        + positions[:, 2:3] * directions[None, :, 2]
    )
    cosine = jnp.cos(phases)
    sine_part = jnp.sin(phases)
    chosen = jnp.einsum("cmt,td->cmd", pattern, select, precision=HIGHEST_PRECISION)
    inc_real = cosine[None] * chosen[0][:, None, :] - sine_part[None] * chosen[1][:, None, :]
    inc_imag = cosine[None] * chosen[1][:, None, :] + sine_part[None] * chosen[0][:, None, :]
    return (inc_real, inc_imag)


def translate(trans_table, classes, block_values):
    item_count = classes.shape[0]
    mode_count = trans_table.shape[2]
    grouped_classes = classes.reshape(item_count // 8, 8)
    grouped_values = block_values.reshape((item_count // 8, 8) + block_values.shape[1:])

    def one_group(group_items):
        picked, values = group_items
        tables = trans_table[picked]
        data_real = values[:, :mode_count]
        data_imag = values[:, mode_count:]
        part_real = jnp.einsum(
            "kij,kjc->kic", tables[:, 0], data_real, preferred_element_type=jnp.float32
        ) - jnp.einsum("kij,kjc->kic", tables[:, 1], data_imag, preferred_element_type=jnp.float32)
        part_imag = jnp.einsum(
            "kij,kjc->kic", tables[:, 1], data_real, preferred_element_type=jnp.float32
        ) + jnp.einsum("kij,kjc->kic", tables[:, 0], data_imag, preferred_element_type=jnp.float32)
        return jnp.concatenate([part_real, part_imag], 1).astype(jnp.bfloat16)

    return lax.map(one_group, (grouped_classes, grouped_values)).reshape(block_values.shape)


def shards(
    positions,
    wave_vectors,
    pattern,
    dir_index,
    mie,
    trans_table,
    pair_route,
    pair_source,
    pair_target,
    pair_class,
):
    mode_count = pattern.shape[1]
    spheres = positions.shape[0]
    directions = dir_index.shape[0]
    columns = BLOCK * directions
    block_count = spheres // BLOCK
    devices = lax.axis_size("sph")
    pair_count = pair_source.shape[0]
    capacity = max(2, 2 * pair_count // devices)
    slot_count = devices * capacity
    inc_real, inc_imag = incident_field(positions, wave_vectors, pattern, dir_index)
    mie_real = mie[0][:, :, None]
    mie_imag = mie[1][:, :, None]
    scat_real = mie_real * inc_real - mie_imag * inc_imag
    scat_imag = mie_real * inc_imag + mie_imag * inc_real
    coeffs = jnp.concatenate([scat_real, scat_imag], 0).astype(jnp.bfloat16)
    block_data = coeffs.reshape(2 * mode_count, block_count, columns).transpose(1, 0, 2)
    dest_device = pair_route[:, 0]
    by_device = (dest_device[:, None] == jnp.arange(devices, dtype=jnp.int32)[None, :]).astype(
        jnp.int32
    )
    before = jnp.cumsum(by_device, axis=0) - by_device
    rank_in = jnp.sum(before * by_device, axis=1)
    slot_of = dest_device * capacity + rank_in
    slot_match = (jnp.arange(slot_count, dtype=jnp.int32)[:, None] == slot_of[None, :]).astype(
        jnp.int32
    )
    filled = jnp.sum(slot_match, axis=1)
    slot_pair = jnp.sum(slot_match * jnp.arange(pair_count, dtype=jnp.int32)[None, :], axis=1)
    slot_target = jnp.where(filled > 0, pair_target[slot_pair], -1)
    keep_slot = filled.astype(jnp.bfloat16)[:, None, None]
    computed = translate(trans_table, pair_class, block_data[pair_source])
    outgoing = computed[slot_pair] * keep_slot
    outgoing = outgoing.reshape(devices, capacity, 2 * mode_count, columns)
    arrived = lax.all_to_all(outgoing, "sph", split_axis=0, concat_axis=0, tiled=True)
    targets = lax.all_to_all(
        slot_target.reshape(devices, capacity), "sph", split_axis=0, concat_axis=0, tiled=True
    ).reshape(slot_count)
    partial_value = arrived.reshape(slot_count, 2 * mode_count, columns)
    gather_matrix = (jnp.arange(block_count, dtype=jnp.int32)[:, None] == targets[None, :]).astype(
        jnp.bfloat16
    )
    summed = jnp.dot(
        gather_matrix,
        partial_value.reshape(slot_count, 2 * mode_count * columns),
        preferred_element_type=jnp.float32,
    )
    summed = (
        summed.reshape(block_count, 2 * mode_count, columns)
        .transpose(1, 0, 2)
        .reshape(2 * mode_count, spheres, directions)
    )
    total_real = inc_real + summed[:mode_count]
    total_imag = inc_imag + summed[mode_count:]
    out_real = mie_real * total_real - mie_imag * total_imag
    out_imag = mie_real * total_imag + mie_imag * total_real
    scattered = (
        jnp.concatenate([out_real, out_imag], 0)
        .reshape(2 * mode_count, spheres * directions)
        .astype(jnp.bfloat16)
    )
    local_ext = jnp.sum(inc_real * out_real + inc_imag * out_imag, axis=(0, 1))
    extinction = lax.psum(local_ext, "sph")
    return (scattered, extinction)


def solution(mesh):
    placed = (
        P("sph", None),
        P(),
        P(),
        P("groups"),
        P(None, None, "sph"),
        P(),
        P("sph", None),
        P("sph"),
        P("sph"),
        P("sph"),
    )
    return jax.shard_map(
        shards,
        mesh=mesh,
        in_specs=placed,
        out_specs=(P(None, ("groups", "sph")), P("groups")),
        check_vma=False,
    )
```

profile of v0, /device:TPU:0, one launch (start us, length us, event | category | flops | bytes accessed | tf_op | source)
XLA Modules:
  0.0 671.2 jit_solution(2450275542576880069)
XLA Ops:
  5.5 7.4 %all-to-all-start = ((s32[16,1,8]{2,1,0:T(1,128)}), s32[16,1,8]{2,1,0:T(1,128)S(1)}, u32[]{:S(2)}, u32[]{:S(2)}) async-start(s32[16,1,8]{2,1,0:T(1,128)} %bitcast.24), calls=%async_computation | async-start | bytes 16384 | tf_op jit(solution)/shard_map/all_to_all | solution.py:97
  21.9 4.3 gather_fusion.2
  26.3 134.5 %while.10 = (s32[]{:T(128)}, bf16[8,8,896,64]{2,3,1,0:T(8,128)(2,1)}, s32[8,8]{1,0:T(8,128)S(1)}, bf16[8,2,448,448]{3,2,1,0:T(8,128)(2,1)}, bf16[8,8,896,64]{2,3,1,0:T(8,128)(2,1)}, /*index=5*/s32[]{:T(128)}) while((s32[]{:T(128)}, bf16[8,8,896,64]{2,3,1,0:T(8,128)(2,1)}, s32[8,8]{1,0:T(8,128)S(1)}, bf16[8,2,448,448]{3,2,1,0:T(8,128)(2,1)}, ...), condition=%wide.region_5.6_spmd, body=%wide.region_4.5_spmd.sunk | while | flops 824837120 | bytes 63836904 | solution.py:48
  26.3 7.0 %gather_fusion = bf16[8,2,448,448]{3,2,1,0:T(8,128)(2,1)} fusion(bf16[8,2,448,448]{3,2,1,0:T(8,128)(2,1)} %get-tuple-element.133, s32[1024]{0:T(1024)S(1)} %pad_clamp_fusion.4), kind=kCustom, calls=%fused_computation.clone.1 | custom fusion | bytes 12845088 | tf_op jit(solution)/shard_map/while/body/eval_jaxpr/gather | solution.py:37
  43.1 7.0 %gather_fusion = bf16[8,2,448,448]{3,2,1,0:T(8,128)(2,1)} fusion(bf16[8,2,448,448]{3,2,1,0:T(8,128)(2,1)} %get-tuple-element.133, s32[1024]{0:T(1024)S(1)} %pad_clamp_fusion.4), kind=kCustom, calls=%fused_computation.clone.1 | custom fusion | bytes 12845088 | tf_op jit(solution)/shard_map/while/body/eval_jaxpr/gather | solution.py:37
  51.5 3.5 fusion.68
  59.9 7.0 %gather_fusion = bf16[8,2,448,448]{3,2,1,0:T(8,128)(2,1)} fusion(bf16[8,2,448,448]{3,2,1,0:T(8,128)(2,1)} %get-tuple-element.133, s32[1024]{0:T(1024)S(1)} %pad_clamp_fusion.4), kind=kCustom, calls=%fused_computation.clone.1 | custom fusion | bytes 12845088 | tf_op jit(solution)/shard_map/while/body/eval_jaxpr/gather | solution.py:37
  68.3 3.5 fusion.68
  76.7 7.0 %gather_fusion = bf16[8,2,448,448]{3,2,1,0:T(8,128)(2,1)} fusion(bf16[8,2,448,448]{3,2,1,0:T(8,128)(2,1)} %get-tuple-element.133, s32[1024]{0:T(1024)S(1)} %pad_clamp_fusion.4), kind=kCustom, calls=%fused_computation.clone.1 | custom fusion | bytes 12845088 | tf_op jit(solution)/shard_map/while/body/eval_jaxpr/gather | solution.py:37
  93.5 7.0 %gather_fusion = bf16[8,2,448,448]{3,2,1,0:T(8,128)(2,1)} fusion(bf16[8,2,448,448]{3,2,1,0:T(8,128)(2,1)} %get-tuple-element.133, s32[1024]{0:T(1024)S(1)} %pad_clamp_fusion.4), kind=kCustom, calls=%fused_computation.clone.1 | custom fusion | bytes 12845088 | tf_op jit(solution)/shard_map/while/body/eval_jaxpr/gather | solution.py:37
  101.9 3.5 fusion.68
  110.3 7.0 %gather_fusion = bf16[8,2,448,448]{3,2,1,0:T(8,128)(2,1)} fusion(bf16[8,2,448,448]{3,2,1,0:T(8,128)(2,1)} %get-tuple-element.133, s32[1024]{0:T(1024)S(1)} %pad_clamp_fusion.4), kind=kCustom, calls=%fused_computation.clone.1 | custom fusion | bytes 12845088 | tf_op jit(solution)/shard_map/while/body/eval_jaxpr/gather | solution.py:37
  127.1 7.0 %gather_fusion = bf16[8,2,448,448]{3,2,1,0:T(8,128)(2,1)} fusion(bf16[8,2,448,448]{3,2,1,0:T(8,128)(2,1)} %get-tuple-element.133, s32[1024]{0:T(1024)S(1)} %pad_clamp_fusion.4), kind=kCustom, calls=%fused_computation.clone.1 | custom fusion | bytes 12845088 | tf_op jit(solution)/shard_map/while/body/eval_jaxpr/gather | solution.py:37
  144.0 7.0 %gather_fusion = bf16[8,2,448,448]{3,2,1,0:T(8,128)(2,1)} fusion(bf16[8,2,448,448]{3,2,1,0:T(8,128)(2,1)} %get-tuple-element.133, s32[1024]{0:T(1024)S(1)} %pad_clamp_fusion.4), kind=kCustom, calls=%fused_computation.clone.1 | custom fusion | bytes 12845088 | tf_op jit(solution)/shard_map/while/body/eval_jaxpr/gather | solution.py:37
  160.7 12.3 %gather_fusion.3 = bf16[128,896,64]{1,2,0:T(8,128)(2,1)} fusion(bf16[64,896,64]{1,2,0:T(8,128)(2,1)} %bitcast.33, s32[1024]{0:T(1024)S(1)} %pad_clamp_fusion.2), kind=kCustom, calls=%fused_computation.3 | custom fusion | bytes 29360640 | tf_op jit(solution)/shard_map/gather | solution.py:94
  173.1 13.5 %broadcast_multiply_fusion = bf16[16,8,896,64]{2,3,1,0:T(8,128)(2,1)} fusion(bf16[16,8,896,64]{2,3,1,0:T(8,128)(2,1)} %bitcast.236, bf16[16,8]{1,0:T(8,128)(2,1)S(1)} %convert_element_type.32), kind=kLoop, calls=%fused_computation.29 | loop fusion | flops 7340032 | bytes 29360384 | tf_op jit(solution)/shard_map/mul | solution.py:94
  186.6 6.0 all-to-all-start.1
  194.7 258.1 %all-to-all-done.1 = bf16[16,8,896,64]{2,3,1,0:T(8,128)(2,1)} async-done(((bf16[16,8,896,64]{2,3,1,0:T(8,128)(2,1)}), bf16[16,8,896,64]{2,3,1,0:T(8,128)(2,1)}, u32[]{:S(2)}, u32[]{:S(2)}) %all-to-all-start.1) | async-done | bytes 14680096 | tf_op jit(solution)/shard_map/all_to_all | solution.py:96
  452.8 26.5 %copy.80 = bf16[16,8,896,64]{3,2,1,0:T(8,128)(2,1)} copy(bf16[16,8,896,64]{2,3,1,0:T(8,128)(2,1)} %all-to-all-done.1) | data formatting | bytes 29360128 | tf_op jit(solution)/shard_map/all_to_all | solution.py:96
  479.3 28.1 %reshape_reshape.3 = bf16[128,57344]{1,0:T(8,128)(2,1)} reshape(bf16[16,8,896,64]{3,2,1,0:T(8,128)(2,1)} %copy.80) | data formatting | bytes 29360128 | tf_op jit(solution)/shard_map/reshape;reshape | solution.py:106
  507.4 20.2 %copy.81 = bf16[57344,128]{1,0:T(8,128)(2,1)} copy(bf16[57344,128]{0,1:T(8,128)(2,1)} %bitcast.238) | data formatting | bytes 29360128 | tf_op jit(solution)/shard_map/dot_general | solution.py:104
  527.6 35.5 %fusion.34 = f32[896,16,64]{0,1,2:T(8,128)} fusion(bf16[896,64,128]{2,1,0:T(8,128)(2,1)} %bitcast.237, s32[128]{0:T(128)S(1)} %eq.64), kind=kOutput, calls=%fused_computation.61 | convolution fusion | flops 234883072 | bytes 18350592 | tf_op jit(solution)/shard_map/dot_general | solution.py:104
  563.1 9.9 %add_reduce_fusion = (f32[16,64]{0,1:T(8,128)S(1)}, f32[448,16,64]{0,1,2:T(8,128)S(1)}, f32[448,16,64]{0,1,2:T(8,128)S(1)}) fusion(f32[448,16,64]{0,2,1:T(8,128)S(1)} %bitcast.241, f32[448,16,64]{0,2,1:T(8,128)} %bitcast.247, f32[448,16,64]{0,2,1:T(8,128)S(1)} %bitcast.243, f32[448,16,64]{0,2,1:T(8,128)S(1)} %bitcast.245, f32[16,64]{0,1:T(8,128)S(1)} %copy.87, ...), kind=kLoop, calls=%fused_computation.60 | loop fusion | flops 8256512 | bytes 14692352 | tf_op jit(solution)/shard_map/reduce_sum | solution.py:123
  580.4 90.4 %psum.7 = f32[32]{0:T(128)} all-reduce(f32[32]{0:T(128)S(1)} %reduce_sum.51), channel_id=1, replica_groups=mesh['groups'=2,'sph'=16] {'sph'}, use_global_device_ids=true, to_apply=%region_8.9 | all-reduce | flops 32 | bytes 256 | tf_op jit(solution)/shard_map/psum | solution.py:124
  (192 shorter events, 90.8 us)
Async XLA Ops:
  0.6 15.6 %copy-start = (f32[2,448,256]{2,1,0:T(8,128)S(1)}, f32[2,448,256]{2,1,0:T(8,128)}, u32[]{:S(2)}) copy-start(f32[2,448,256]{2,1,0:T(8,128)} %param.14) | copy-start | bytes 2752516
  0.6 16.9 %copy-start.20 = (s32[64]{0:T(128)S(1)}, s32[64]{0:T(128)}, u32[]{:S(2)}) copy-start(s32[64]{0:T(128)} %param.19) | copy-start | bytes 772
  0.7 16.9 %copy-start.19 = (s32[64]{0:T(128)S(1)}, s32[64]{0:T(128)}, u32[]{:S(2)}) copy-start(s32[64]{0:T(128)} %param.21) | copy-start | bytes 772
  0.7 17.0 %copy-start.18 = (f32[2,448,32]{1,2,0:T(8,128)S(1)}, f32[2,448,32]{1,2,0:T(8,128)}, u32[]{:S(2)}) copy-start(f32[2,448,32]{1,2,0:T(8,128)} %param.16) | copy-start | bytes 344068
  5.5 181.1 %all-to-all-start = ((s32[16,1,8]{2,1,0:T(1,128)}), s32[16,1,8]{2,1,0:T(1,128)S(1)}, u32[]{:S(2)}, u32[]{:S(2)}) async-start(s32[16,1,8]{2,1,0:T(1,128)} %bitcast.24), calls=%async_computation | async-start | bytes 16384 | tf_op jit(solution)/shard_map/all_to_all | solution.py:97
  18.0 1.3 copy-start.3
  18.3 1.7 copy-start.5
  18.6 2.5 copy-start.7
  18.9 2.5 copy-start.9
  33.3 4.9 copy-start.2
  50.1 4.9 copy-start.2
  66.9 4.9 copy-start.2
  83.7 4.9 copy-start.2
  100.5 4.9 copy-start.2
  117.3 4.9 copy-start.2
  134.1 4.9 copy-start.2
  151.0 4.9 copy-start.2
  186.6 266.2 %all-to-all-start.1 = ((bf16[16,8,896,64]{2,3,1,0:T(8,128)(2,1)}), bf16[16,8,896,64]{2,3,1,0:T(8,128)(2,1)}, u32[]{:S(2)}, u32[]{:S(2)}) async-start(bf16[16,8,896,64]{2,3,1,0:T(8,128)(2,1)} %broadcast_multiply_fusion), calls=%async_computation.1 | async-start | bytes 29360128 | tf_op jit(solution)/shard_map/all_to_all | solution.py:96
  527.6 35.5 %copy-start.4 = (f32[448,32,32]{0,2,1:T(8,128)S(1)}, f32[448,32,32]{0,2,1:T(8,128)}, u32[]{:S(2)}) copy-start(f32[448,32,32]{0,2,1:T(8,128)} %copy-done.3) | copy-start | bytes 5505028
  527.6 35.5 %copy-start.6 = (f32[448,32,32]{0,2,1:T(8,128)S(1)}, f32[448,32,32]{0,2,1:T(8,128)}, u32[]{:S(2)}) copy-start(f32[448,32,32]{0,2,1:T(8,128)} %copy-done.5) | copy-start | bytes 5505028
  527.6 35.5 %copy-start.8 = (f32[448,32,32]{0,2,1:T(8,128)S(1)}, f32[448,32,32]{0,2,1:T(8,128)}, u32[]{:S(2)}) copy-start(f32[448,32,32]{0,2,1:T(8,128)} %copy-done.7) | copy-start | bytes 5505028
  574.3 1.3 copy-start.11
  574.3 1.3 copy-start.13
  577.2 93.6 %copy-start.1 = (f32[2,448,256]{2,1,0:T(8,128)S(1)}, f32[2,448,256]{2,1,0:T(8,128)}, u32[]{:S(2)}) copy-start(f32[2,448,256]{2,1,0:T(8,128)} %param.14) | copy-start | bytes 2752516
  (6 other events, 5.3 us)
where the time goes:
time: 683 us; the launch traced here: 671 us
  waiting for transfers between devices  258 us (38%)
  local copies, waits for them, and re-layouts  172 us (25%)
  matrix products  94.1 us (14%)
  blocking collectives  90.4 us (13%)
  other arithmetic  41 us (6%)
  starting transfers between devices  13.5 us (2%)
    all_to_all x1, waiting for transfers between devices, shards(): lax.all_to_all(outgoing, 'sph', split_axis=0, concat_axis=0, tiled=True)  258 us
    psum x1, blocking collectives, shards(): extinction = lax.psum(local_ext, 'sph')  90.4 us
    gather x8, local copies, waits for them, and re-layouts, one_group(): tables = trans_table[picked]  56.2 us
    dot_general x1, matrix products, shards(): jnp.dot(gather_matrix, partial_value.reshape(slot_count, 2 * mode_count *...  35.5 us
    another operation x1, local copies, waits for them, and re-layouts, shards(): partial_value.reshape(slot_count, 2 * mode_count * columns)  28.1 us
    dot_general x8, matrix products, one_group(): jnp.einsum('kij,kjc->kic', tables[:, 0], data_real, preferred_element_typ...  27.6 us
    all_to_all x1, local copies, waits for them, and re-layouts, shards(): lax.all_to_all(outgoing, 'sph', split_axis=0, concat_axis=0, tiled=True)  26.5 us
    dot_general x1, local copies, waits for them, and re-layouts, shards(): jnp.dot(gather_matrix, partial_value.reshape(slot_count, 2 * mode_count *...  20.2 us
  transfers between devices with their start and end apart: 2, of which 1 were waited for; matrix products, arithmetic and copies ran while one was open for 26% of the time, Pallas kernels for 0%

commit v1 on v0

--- a/solution.py
+++ b/solution.py
@@ -5,6 +5,29 @@
 
 BLOCK = 2
 HIGHEST_PRECISION = lax.Precision.HIGHEST
+
+
+def in_blocks(value, dim, devices):
+    before, after = (value.shape[:dim], value.shape[dim + 1 :])
+    return jnp.moveaxis(value.reshape(*before, devices, -1, *after), dim, 0)
+
+
+def in_order(blocks, dim):
+    blocks = jnp.moveaxis(blocks, 0, dim)
+    lengths = blocks.shape
+    return blocks.reshape(*lengths[:dim], lengths[dim] * lengths[dim + 1], *lengths[dim + 2 :])
+
+
+def rotated_exchange(shard, axis, split_dim, concat_dim):
+    length, index = (lax.axis_size(axis), lax.axis_index(axis))
+    blocks = in_blocks(shard, split_dim, length)
+    result = blocks
+    for lap in range(1, length):
+        target, source = ((index + lap) % length, (index - lap) % length)
+        sent = lax.dynamic_index_in_dim(blocks, target, 0)
+        partner_block = lax.ppermute(sent, axis, [(i, (i + lap) % length) for i in range(length)])
+        result = lax.dynamic_update_slice_in_dim(result, partner_block, source, axis=0)
+    return in_order(result, concat_dim)
 
 
 def incident_field(positions, wave_vectors, pattern, dir_index):
@@ -93,7 +116,7 @@
     computed = translate(trans_table, pair_class, block_data[pair_source])
     outgoing = computed[slot_pair] * keep_slot
     outgoing = outgoing.reshape(devices, capacity, 2 * mode_count, columns)
-    arrived = lax.all_to_all(outgoing, "sph", split_axis=0, concat_axis=0, tiled=True)
+    arrived = rotated_exchange(outgoing, "sph", 0, 0)
     targets = lax.all_to_all(
         slot_target.reshape(devices, capacity), "sph", split_axis=0, concat_axis=0, tiled=True
     ).reshape(slot_count)

time: 683 us -> 755 us (1.11)
  starting transfers between devices: 13.5 us -> 63.6 us
  blocking collectives: 90.4 us -> 48.5 us
  local copies, waits for them, and re-layouts: 172 us -> 210 us
  waiting for transfers between devices: 258 us -> 283 us
  matrix products: 94.1 us -> 103 us
    all_to_all x1 -> x0, waiting for transfers between devices: 258 us -> none  [shards(): lax.all_to_all(outgoing, 'sph', split_axis=0, concat_axis=0, tiled=True)]
    ppermute x0 -> x15, waiting for transfers between devices: none -> 205 us  [rotated_exchange(): lax.ppermute(sent, axis, [(i, (i + lap) % length) for i in range(length)])]
    all_to_all x1, waiting for transfers between devices: 0.01 us -> 78 us  [shards(): lax.all_to_all(slot_target.reshape(devices, capacity), 'sph', split_axis=...]
    dynamic_update_slice x0 -> x15, local copies, waits for them, and re-layouts: none -> 47 us  [rotated_exchange(): lax.dynamic_update_slice_in_dim(result, partner_block, source, axis=0)]
    psum x1, blocking collectives: 90.4 us -> 48.5 us  [shards(): extinction = lax.psum(local_ext, 'sph')]
    ppermute x0 -> x15, starting transfers between devices: none -> 39.6 us  [rotated_exchange(): lax.ppermute(sent, axis, [(i, (i + lap) % length) for i in range(length)])]
    all_to_all x1 -> x0, local copies, waits for them, and re-layouts: 26.5 us -> none  [shards(): lax.all_to_all(outgoing, 'sph', split_axis=0, concat_axis=0, tiled=True)]
    all_to_all x1, starting transfers between devices: 7.41 us -> 24 us  [shards(): lax.all_to_all(slot_target.reshape(devices, capacity), 'sph', split_axis=...]
  transfers between devices with their start and end apart: 2 -> 16, of which waited for: 1 -> 10; matrix products, arithmetic and copies ran while one was open for 26% -> 3% of each run, Pallas kernels for 0% -> 0%
where the time goes in v1:
time: 755 us; the launch traced here: 744 us
  waiting for transfers between devices  283 us (37%)
  local copies, waits for them, and re-layouts  210 us (28%)
  matrix products  103 us (14%)
  starting transfers between devices  63.6 us (8%)
  blocking collectives  48.5 us (6%)
  other arithmetic  34.2 us (5%)
    ppermute x15, waiting for transfers between devices, rotated_exchange(): lax.ppermute(sent, axis, [(i, (i + lap) % length) for i in range(length)])  205 us
    all_to_all x1, waiting for transfers between devices, shards(): lax.all_to_all(slot_target.reshape(devices, capacity), 'sph', split_axis=...  78 us
    gather x8, local copies, waits for them, and re-layouts, one_group(): tables = trans_table[picked]  57 us
    psum x1, blocking collectives, shards(): extinction = lax.psum(local_ext, 'sph')  48.5 us
    dynamic_update_slice x15, local copies, waits for them, and re-layouts, rotated_exchange(): lax.dynamic_update_slice_in_dim(result, partner_block, source, axis=0)  47 us
    dot_general x1, matrix products, shards(): jnp.dot(gather_matrix, partial_value.reshape(slot_count, 2 * mode_count *...  44 us
    ppermute x15, starting transfers between devices, rotated_exchange(): lax.ppermute(sent, axis, [(i, (i + lap) % length) for i in range(length)])  39.6 us
    another operation x1, local copies, waits for them, and re-layouts, shards(): partial_value.reshape(slot_count, 2 * mode_count * columns)  28.1 us
  transfers between devices with their start and end apart: 16, of which 10 were waited for; matrix products, arithmetic and copies ran while one was open for 3% of the time, Pallas kernels for 0%

profile of v1, /device:TPU:0, one launch (start us, length us, event | category | flops | bytes accessed | tf_op | source)
XLA Modules:
  0.0 744.4 jit_solution(5941822594320126913)
XLA Ops:
  16.1 135.3 %while.10 = (s32[]{:T(128)}, bf16[8,8,896,64]{2,3,1,0:T(8,128)(2,1)}, s32[8,8]{1,0:T(8,128)S(1)}, bf16[8,2,448,448]{3,2,1,0:T(8,128)(2,1)}, bf16[8,8,896,64]{2,3,1,0:T(8,128)(2,1)}, /*index=5*/s32[]{:T(128)}) while((s32[]{:T(128)}, bf16[8,8,896,64]{2,3,1,0:T(8,128)(2,1)}, s32[8,8]{1,0:T(8,128)S(1)}, bf16[8,2,448,448]{3,2,1,0:T(8,128)(2,1)}, ...), condition=%wide.region_5.6_spmd, body=%wide.region_4.5_spmd.sunk | while | flops 824837120 | bytes 63836904 | solution.py:71
  16.2 7.1 gather_fusion
  33.1 7.1 gather_fusion
  66.9 7.1 gather_fusion
  151.9 12.3 %gather_fusion.3 = bf16[128,896,64]{1,2,0:T(8,128)(2,1)} fusion(bf16[64,896,64]{1,2,0:T(8,128)(2,1)} %bitcast.33, s32[1024]{0:T(1024)S(1)} %pad_clamp_fusion.2), kind=kCustom, calls=%fused_computation.3 | custom fusion | bytes 29360640 | tf_op jit(solution)/shard_map/gather | solution.py:117
  165.6 8.1 %broadcast_multiply_fusion = bf16[16,1,8,896,64]{3,4,2,1,0:T(8,128)(2,1)S(1)} fusion(bf16[16,1,8,896,64]{3,4,2,1,0:T(8,128)(2,1)} %bitcast.238, bf16[16,8]{1,0:T(8,128)(2,1)S(1)} %convert_element_type.32), kind=kLoop, calls=%fused_computation.29 | loop fusion | flops 7340032 | bytes 29360384 | tf_op jit(solution)/shard_map/mul | solution.py:117
  179.5 16.1 %collective-permute-done = bf16[1,1,8,896,64]{3,4,2,1,0:T(8,128)(2,1)S(1)} collective-permute-done((bf16[1,1,8,896,64]{3,4,2,1,0:T(8,128)(2,1)S(1)}, bf16[1,1,8,896,64]{3,4,2,1,0:T(8,128)(2,1)S(1)}, u32[]{:S(2)}, u32[]{:S(2)}) %collective-permute-start) | collective-permute-done | bytes 917536 | tf_op jit(solution)/shard_map/ppermute | solution.py:28
  195.6 9.1 %constant_dynamic-slice_fusion.1 = (bf16[1,1,8,896,64]{3,4,2,1,0:T(8,128)(2,1)}, bf16[1,1,8,896,64]{3,4,2,1,0:T(8,128)(2,1)}, bf16[1,1,8,896,64]{3,4,2,1,0:T(8,1...) fusion(bf16[16,1,8,896,64]{3,4,2,1,0:T(8,128)(2,1)} %copy-done., ...), kind=kLoop, calls=%fused_computation.84 | loop fusion | bytes 27525180 | tf_op jit(solution)/shard_map/jit(dynamic_index_in_dim)/dynamic_slice | solution.py:27
  210.5 20.2 %collective-permute-done.1 = bf16[1,1,8,896,64]{3,4,2,1,0:T(8,128)(2,1)S(1)} collective-permute-done((bf16[1,1,8,896,64]{3,4,2,1,0:T(8,128)(2,1)S(1)}, bf16[1,1,8,896,64]{3,4,2,1,0:T(8,128)(2,1)S(1)}, u32[]{:S(2)}, u32[]{:S(2)}) %collective-permute-start.1) | collective-permute-done | bytes 917536 | tf_op jit(solution)/shard_map/ppermute | solution.py:28
  236.3 17.1 %collective-permute-start.8 = (bf16[1,1,8,896,64]{3,4,2,1,0:T(8,128)(2,1)}, bf16[1,1,8,896,64]{3,4,2,1,0:T(8,128)(2,1)S(1)}, u32[]{:S(2)}, u32[]{:S(2)}) collective-permute-start(bf16[1,1,8,896,64]{3,4,2,1,0:T(8,128)(2,1)} %get-tuple-element.70), channel_id=1, source_target_pairs={{0,9},{1,10},{2,11},{3,12},{4,13},{5,14},{6,15},{7,0},{8,1},{9,2},... | collective-permute-start | bytes 2752520 | tf_op jit(solution)/shard_map/ppermute | solution.py:28
  254.1 24.0 %all-to-all-start = ((s32[16,1,8]{2,1,0:T(1,128)}), s32[16,1,8]{2,1,0:T(1,128)S(1)}, u32[]{:S(2)}, u32[]{:S(2)}) async-start(s32[16,1,8]{2,1,0:T(1,128)} %bitcast.24), calls=%async_computation | async-start | bytes 16384 | tf_op jit(solution)/shard_map/all_to_all | solution.py:120
  278.5 95.6 %collective-permute-done.4 = bf16[1,1,8,896,64]{3,4,2,1,0:T(8,128)(2,1)} collective-permute-done((bf16[1,1,8,896,64]{3,4,2,1,0:T(8,128)(2,1)}, bf16[1,1,8,896,64]{3,4,2,1,0:T(8,128)(2,1)}, u32[]{:S(2)}, u32[]{:S(2)}) %collective-permute-start.4) | collective-permute-done | bytes 917536 | tf_op jit(solution)/shard_map/ppermute | solution.py:28
  374.8 78.0 %all-to-all-done = s32[16,1,8]{2,1,0:T(1,128)S(1)} async-done(((s32[16,1,8]{2,1,0:T(1,128)}), s32[16,1,8]{2,1,0:T(1,128)S(1)}, u32[]{:S(2)}, u32[]{:S(2)}) %all-to-all-start) | async-done | bytes 544 | tf_op jit(solution)/shard_map/all_to_all | solution.py:120
  458.8 10.2 %collective-permute-start.10 = (bf16[1,1,8,896,64]{3,4,2,1,0:T(8,128)(2,1)S(1)}, bf16[1,1,8,896,64]{3,4,2,1,0:T(8,128)(2,1)S(1)}, u32[]{:S(2)}, u32[]{:S(2)}) collective-permute-start(bf16[1,1,8,896,64]{3,4,2,1,0:T(8,128)(2,1)S(1)} %copy-done.20), channel_id=1, source_target_pairs={{0,11},{1,12},{2,13},{3,14},{4,15},{5,0},{6,1},{7,2},{8,3},{9,4},{... | collective-permute-start | bytes 2752520 | tf_op jit(solution)/shard_map/ppermute | solution.py:28
  490.0 18.6 %collective-permute-done.11 = bf16[1,1,8,896,64]{3,4,2,1,0:T(8,128)(2,1)S(1)} collective-permute-done((bf16[1,1,8,896,64]{3,4,2,1,0:T(8,128)(2,1)S(1)}, bf16[1,1,8,896,64]{3,4,2,1,0:T(8,128)(2,1)S(1)}, u32[]{:S(2)}, u32[]{:S(2)}) %collective-permute-start.11) | collective-permute-done | bytes 917536 | tf_op jit(solution)/shard_map/ppermute | solution.py:28
  509.6 18.6 %collective-permute-done.12 = bf16[1,1,8,896,64]{3,4,2,1,0:T(8,128)(2,1)S(1)} collective-permute-done((bf16[1,1,8,896,64]{3,4,2,1,0:T(8,128)(2,1)S(1)}, bf16[1,1,8,896,64]{3,4,2,1,0:T(8,128)(2,1)S(1)}, u32[]{:S(2)}, u32[]{:S(2)}) %collective-permute-start.12) | collective-permute-done | bytes 917536 | tf_op jit(solution)/shard_map/ppermute | solution.py:28
  529.3 18.6 %collective-permute-done.13 = bf16[1,1,8,896,64]{3,4,2,1,0:T(8,128)(2,1)S(1)} collective-permute-done((bf16[1,1,8,896,64]{3,4,2,1,0:T(8,128)(2,1)S(1)}, bf16[1,1,8,896,64]{3,4,2,1,0:T(8,128)(2,1)S(1)}, u32[]{:S(2)}, u32[]{:S(2)}) %collective-permute-start.13) | collective-permute-done | bytes 917536 | tf_op jit(solution)/shard_map/ppermute | solution.py:28
  549.0 9.6 %collective-permute-done.14 = bf16[1,1,8,896,64]{3,4,2,1,0:T(8,128)(2,1)S(1)} collective-permute-done((bf16[1,1,8,896,64]{3,4,2,1,0:T(8,128)(2,1)S(1)}, bf16[1,1,8,896,64]{3,4,2,1,0:T(8,128)(2,1)S(1)}, u32[]{:S(2)}, u32[]{:S(2)}) %collective-permute-start.14) | collective-permute-done | bytes 917536 | tf_op jit(solution)/shard_map/ppermute | solution.py:28
  559.6 26.5 %copy.80 = bf16[16,1,8,896,64]{4,3,2,0,1:T(8,128)(2,1)} copy(bf16[16,1,8,896,64]{3,4,2,1,0:T(8,128)(2,1)} %constant_dynamic-update-slice_fusion.14) | data formatting | bytes 29360128 | tf_op jit(solution)/shard_map/dynamic_update_slice | solution.py:29
  586.1 28.1 %reshape_reshape_reshape.3 = bf16[128,57344]{1,0:T(8,128)(2,1)} reshape(bf16[16,1,8,896,64]{4,3,2,0,1:T(8,128)(2,1)} %copy.80) | data formatting | bytes 29360128 | tf_op jit(solution)/shard_map/reshape;reshape;reshape | solution.py:129
  614.2 19.9 %copy.81 = bf16[57344,128]{1,0:T(8,128)(2,1)} copy(bf16[57344,128]{0,1:T(8,128)(2,1)} %bitcast.240) | data formatting | bytes 29360128 | tf_op jit(solution)/shard_map/dot_general | solution.py:127
  634.1 44.0 %fusion.34 = f32[896,16,64]{0,1,2:T(8,128)} fusion(bf16[896,64,128]{2,1,0:T(8,128)(2,1)} %bitcast.239, s32[128]{0:T(128)S(1)} %eq.95), kind=kOutput, calls=%fused_computation.61 | convolution fusion | flops 234883072 | bytes 18350592 | tf_op jit(solution)/shard_map/dot_general | solution.py:127
  678.2 9.9 %add_reduce_fusion = (f32[16,64]{0,1:T(8,128)S(1)}, f32[448,16,64]{0,1,2:T(8,128)S(1)}, f32[448,16,64]{0,1,2:T(8,128)S(1)}) fusion(f32[448,16,64]{0,2,1:T(8,128)S(1)} %bitcast.243, f32[448,16,64]{0,2,1:T(8,128)} %bitcast.249, f32[448,16,64]{0,2,1:T(8,128)S(1)} %bitcast.245, f32[448,16,64]{0,2,1:T(8,128)S(1)} %bitcast.247, f32[16,64]{0,1:T(8,128)S(1)} %copy.87, ...), kind=kLoop, calls=%fused_computation.60 | loop fusion | flops 8256512 | bytes 14692352 | tf_op jit(solution)/shard_map/reduce_sum | solution.py:146
  695.5 48.5 %psum.7 = f32[32]{0:T(128)} all-reduce(f32[32]{0:T(128)S(1)} %reduce_sum.51), channel_id=1, replica_groups=mesh['groups'=2,'sph'=16] {'sph'}, use_global_device_ids=true, to_apply=%region_8.9 | all-reduce | flops 32 | bytes 256 | tf_op jit(solution)/shard_map/psum | solution.py:147
  (254 shorter events, 187.7 us)
Async XLA Ops:
  16.1 135.3 %copy-start.29 = (s32[64,1]{0,1:T(1,128)S(1)}, s32[64,1]{0,1:T(1,128)}, u32[]{:S(2)}) copy-start(s32[64,1]{0,1:T(1,128)} %param.18) | copy-start | bytes 772
  179.0 16.6 %collective-permute-start = (bf16[1,1,8,896,64]{3,4,2,1,0:T(8,128)(2,1)S(1)}, bf16[1,1,8,896,64]{3,4,2,1,0:T(8,128)(2,1)S(1)}, u32[]{:S(2)}, u32[]{:S(2)}) collective-permute-start(bf16[1,1,8,896,64]{3,4,2,1,0:T(8,128)(2,1)S(1)} %constant_dynamic-slice_fusion.15), channel_id=1, source_target_pairs={{0,1},{1,2},{2,3},{3,4},{4,5},{5,6},{6,7},{7,8},{8,9},{9,10},{10,1... | collective-permute-start | bytes 2752520 | tf_op jit(solution)/shard_map/ppermute | solution.py:28
  204.7 26.1 %collective-permute-start.1 = (bf16[1,1,8,896,64]{3,4,2,1,0:T(8,128)(2,1)S(1)}, bf16[1,1,8,896,64]{3,4,2,1,0:T(8,128)(2,1)S(1)}, u32[]{:S(2)}, u32[]{:S(2)}) collective-permute-start(bf16[1,1,8,896,64]{3,4,2,1,0:T(8,128)(2,1)S(1)} %get-tuple-element.77), channel_id=1, source_target_pairs={{0,2},{1,3},{2,4},{3,5},{4,6},{5,7},{6,8},{7,9},{8,10},{9,11},{10,... | collective-permute-start | bytes 2752520 | tf_op jit(solution)/shard_map/ppermute | solution.py:28
  204.7 28.0 %collective-permute-start.2 = (bf16[1,1,8,896,64]{3,4,2,1,0:T(8,128)(2,1)S(1)}, bf16[1,1,8,896,64]{3,4,2,1,0:T(8,128)(2,1)S(1)}, u32[]{:S(2)}, u32[]{:S(2)}) collective-permute-start(bf16[1,1,8,896,64]{3,4,2,1,0:T(8,128)(2,1)S(1)} %get-tuple-element.76), channel_id=1, source_target_pairs={{0,3},{1,4},{2,5},{3,6},{4,7},{5,8},{6,9},{7,10},{8,11},{9,12},{10... | collective-permute-start | bytes 2752520 | tf_op jit(solution)/shard_map/ppermute | solution.py:28
  204.8 30.5 %collective-permute-start.3 = (bf16[1,1,8,896,64]{3,4,2,1,0:T(8,128)(2,1)S(1)}, bf16[1,1,8,896,64]{3,4,2,1,0:T(8,128)(2,1)S(1)}, u32[]{:S(2)}, u32[]{:S(2)}) collective-permute-start(bf16[1,1,8,896,64]{3,4,2,1,0:T(8,128)(2,1)S(1)} %get-tuple-element.75), channel_id=1, source_target_pairs={{0,4},{1,5},{2,6},{3,7},{4,8},{5,9},{6,10},{7,11},{8,12},{9,13},{1... | collective-permute-start | bytes 2752520 | tf_op jit(solution)/shard_map/ppermute | solution.py:28
  205.6 168.5 %collective-permute-start.4 = (bf16[1,1,8,896,64]{3,4,2,1,0:T(8,128)(2,1)}, bf16[1,1,8,896,64]{3,4,2,1,0:T(8,128)(2,1)}, u32[]{:S(2)}, u32[]{:S(2)}) collective-permute-start(bf16[1,1,8,896,64]{3,4,2,1,0:T(8,128)(2,1)} %get-tuple-element.74), channel_id=1, source_target_pairs={{0,5},{1,6},{2,7},{3,8},{4,9},{5,10},{6,11},{7,12},{8,13},{9,14},{... | collective-permute-start | bytes 2752520 | tf_op jit(solution)/shard_map/ppermute | solution.py:28
  208.2 250.6 %collective-permute-start.5 = (bf16[1,1,8,896,64]{3,4,2,1,0:T(8,128)(2,1)}, bf16[1,1,8,896,64]{3,4,2,1,0:T(8,128)(2,1)}, u32[]{:S(2)}, u32[]{:S(2)}) collective-permute-start(bf16[1,1,8,896,64]{3,4,2,1,0:T(8,128)(2,1)} %get-tuple-element.73), channel_id=1, source_target_pairs={{0,6},{1,7},{2,8},{3,9},{4,10},{5,11},{6,12},{7,13},{8,14},{9,15},... | collective-permute-start | bytes 2752520 | tf_op jit(solution)/shard_map/ppermute | solution.py:28
  230.7 239.2 %collective-permute-start.6 = (bf16[1,1,8,896,64]{3,4,2,1,0:T(8,128)(2,1)}, bf16[1,1,8,896,64]{3,4,2,1,0:T(8,128)(2,1)S(1)}, u32[]{:S(2)}, u32[]{:S(2)}) collective-permute-start(bf16[1,1,8,896,64]{3,4,2,1,0:T(8,128)(2,1)} %get-tuple-element.72), channel_id=1, source_target_pairs={{0,7},{1,8},{2,9},{3,10},{4,11},{5,12},{6,13},{7,14},{8,15},{9,0},... | collective-permute-start | bytes 2752520 | tf_op jit(solution)/shard_map/ppermute | solution.py:28
  232.8 240.9 %collective-permute-start.7 = (bf16[1,1,8,896,64]{3,4,2,1,0:T(8,128)(2,1)}, bf16[1,1,8,896,64]{3,4,2,1,0:T(8,128)(2,1)S(1)}, u32[]{:S(2)}, u32[]{:S(2)}) collective-permute-start(bf16[1,1,8,896,64]{3,4,2,1,0:T(8,128)(2,1)} %get-tuple-element.71), channel_id=1, source_target_pairs={{0,8},{1,9},{2,10},{3,11},{4,12},{5,13},{6,14},{7,15},{8,0},{9,1},... | collective-permute-start | bytes 2752520 | tf_op jit(solution)/shard_map/ppermute | solution.py:28
  236.3 239.9 %collective-permute-start.8 = (bf16[1,1,8,896,64]{3,4,2,1,0:T(8,128)(2,1)}, bf16[1,1,8,896,64]{3,4,2,1,0:T(8,128)(2,1)S(1)}, u32[]{:S(2)}, u32[]{:S(2)}) collective-permute-start(bf16[1,1,8,896,64]{3,4,2,1,0:T(8,128)(2,1)} %get-tuple-element.70), channel_id=1, source_target_pairs={{0,9},{1,10},{2,11},{3,12},{4,13},{5,14},{6,15},{7,0},{8,1},{9,2},... | collective-permute-start | bytes 2752520 | tf_op jit(solution)/shard_map/ppermute | solution.py:28
  254.1 198.7 %all-to-all-start = ((s32[16,1,8]{2,1,0:T(1,128)}), s32[16,1,8]{2,1,0:T(1,128)S(1)}, u32[]{:S(2)}, u32[]{:S(2)}) async-start(s32[16,1,8]{2,1,0:T(1,128)} %bitcast.24), calls=%async_computation | async-start | bytes 16384 | tf_op jit(solution)/shard_map/all_to_all | solution.py:120
  374.1 103.6 %collective-permute-start.9 = (bf16[1,1,8,896,64]{3,4,2,1,0:T(8,128)(2,1)}, bf16[1,1,8,896,64]{3,4,2,1,0:T(8,128)(2,1)}, u32[]{:S(2)}, u32[]{:S(2)}) collective-permute-start(bf16[1,1,8,896,64]{3,4,2,1,0:T(8,128)(2,1)} %get-tuple-element.69), channel_id=1, source_target_pairs={{0,10},{1,11},{2,12},{3,13},{4,14},{5,15},{6,0},{7,1},{8,2},{9,3},... | collective-permute-start | bytes 2752520 | tf_op jit(solution)/shard_map/ppermute | solution.py:28
  454.1 19.6 %copy-start.18 = (bf16[1,1,8,896,64]{3,4,2,1,0:T(8,128)(2,1)S(1)}, bf16[1,1,8,896,64]{3,4,2,1,0:T(8,128)(2,1)}, u32[]{:S(2)}) copy-start(bf16[1,1,8,896,64]{3,4,2,1,0:T(8,128)(2,1)} %get-tuple-element.66) | copy-start | bytes 2752516
  456.4 19.7 %copy-start.17 = (bf16[1,1,8,896,64]{3,4,2,1,0:T(8,128)(2,1)S(1)}, bf16[1,1,8,896,64]{3,4,2,1,0:T(8,128)(2,1)}, u32[]{:S(2)}) copy-start(bf16[1,1,8,896,64]{3,4,2,1,0:T(8,128)(2,1)} %get-tuple-element.65) | copy-start | bytes 2752516
  458.8 19.0 %copy-start.16 = (bf16[1,1,8,896,64]{3,4,2,1,0:T(8,128)(2,1)S(1)}, bf16[1,1,8,896,64]{3,4,2,1,0:T(8,128)(2,1)}, u32[]{:S(2)}) copy-start(bf16[1,1,8,896,64]{3,4,2,1,0:T(8,128)(2,1)} %get-tuple-element.64) | copy-start | bytes 2752516
  458.8 30.2 %collective-permute-start.10 = (bf16[1,1,8,896,64]{3,4,2,1,0:T(8,128)(2,1)S(1)}, bf16[1,1,8,896,64]{3,4,2,1,0:T(8,128)(2,1)S(1)}, u32[]{:S(2)}, u32[]{:S(2)}) collective-permute-start(bf16[1,1,8,896,64]{3,4,2,1,0:T(8,128)(2,1)S(1)} %copy-done.20), channel_id=1, source_target_pairs={{0,11},{1,12},{2,13},{3,14},{4,15},{5,0},{6,1},{7,2},{8,3},{9,4},{... | collective-permute-start | bytes 2752520 | tf_op jit(solution)/shard_map/ppermute | solution.py:28
  470.0 38.6 %collective-permute-start.11 = (bf16[1,1,8,896,64]{3,4,2,1,0:T(8,128)(2,1)S(1)}, bf16[1,1,8,896,64]{3,4,2,1,0:T(8,128)(2,1)S(1)}, u32[]{:S(2)}, u32[]{:S(2)}) collective-permute-start(bf16[1,1,8,896,64]{3,4,2,1,0:T(8,128)(2,1)S(1)} %copy-done.19), channel_id=1, source_target_pairs={{0,12},{1,13},{2,14},{3,15},{4,0},{5,1},{6,2},{7,3},{8,4},{9,5},{1... | collective-permute-start | bytes 2752520 | tf_op jit(solution)/shard_map/ppermute | solution.py:28
  473.7 54.6 %collective-permute-start.12 = (bf16[1,1,8,896,64]{3,4,2,1,0:T(8,128)(2,1)S(1)}, bf16[1,1,8,896,64]{3,4,2,1,0:T(8,128)(2,1)S(1)}, u32[]{:S(2)}, u32[]{:S(2)}) collective-permute-start(bf16[1,1,8,896,64]{3,4,2,1,0:T(8,128)(2,1)S(1)} %copy-done.18), channel_id=1, source_target_pairs={{0,13},{1,14},{2,15},{3,0},{4,1},{5,2},{6,3},{7,4},{8,5},{9,6},{10... | collective-permute-start | bytes 2752520 | tf_op jit(solution)/shard_map/ppermute | solution.py:28
  476.2 71.8 %collective-permute-start.13 = (bf16[1,1,8,896,64]{3,4,2,1,0:T(8,128)(2,1)S(1)}, bf16[1,1,8,896,64]{3,4,2,1,0:T(8,128)(2,1)S(1)}, u32[]{:S(2)}, u32[]{:S(2)}) collective-permute-start(bf16[1,1,8,896,64]{3,4,2,1,0:T(8,128)(2,1)S(1)} %copy-done.17), channel_id=1, source_target_pairs={{0,14},{1,15},{2,0},{3,1},{4,2},{5,3},{6,4},{7,5},{8,6},{9,7},{10,... | collective-permute-start | bytes 2752520 | tf_op jit(solution)/shard_map/ppermute | solution.py:28
  477.8 80.8 %collective-permute-start.14 = (bf16[1,1,8,896,64]{3,4,2,1,0:T(8,128)(2,1)S(1)}, bf16[1,1,8,896,64]{3,4,2,1,0:T(8,128)(2,1)S(1)}, u32[]{:S(2)}, u32[]{:S(2)}) collective-permute-start(bf16[1,1,8,896,64]{3,4,2,1,0:T(8,128)(2,1)S(1)} %copy-done.16), channel_id=1, source_target_pairs={{0,15},{1,0},{2,1},{3,2},{4,3},{5,4},{6,5},{7,6},{8,7},{9,8},{10,9... | collective-permute-start | bytes 2752520 | tf_op jit(solution)/shard_map/ppermute | solution.py:28
  634.1 44.1 %copy-start.6 = (f32[448,32,32]{0,2,1:T(8,128)S(1)}, f32[448,32,32]{0,2,1:T(8,128)}, u32[]{:S(2)}) copy-start(f32[448,32,32]{0,2,1:T(8,128)} %copy-done.5) | copy-start | bytes 5505028
  634.1 44.1 %copy-start.8 = (f32[448,32,32]{0,2,1:T(8,128)S(1)}, f32[448,32,32]{0,2,1:T(8,128)}, u32[]{:S(2)}) copy-start(f32[448,32,32]{0,2,1:T(8,128)} %copy-done.7) | copy-start | bytes 5505028
  634.1 44.1 %copy-start.10 = (f32[448,32,32]{0,2,1:T(8,128)S(1)}, f32[448,32,32]{0,2,1:T(8,128)}, u32[]{:S(2)}) copy-start(f32[448,32,32]{0,2,1:T(8,128)} %copy-done.9) | copy-start | bytes 5505028
  692.3 51.7 %copy-start.1 = (f32[2,448,256]{2,1,0:T(8,128)S(1)}, f32[2,448,256]{2,1,0:T(8,128)}, u32[]{:S(2)}) copy-start(f32[2,448,256]{2,1,0:T(8,128)} %param.14) | copy-start | bytes 2752516
  (29 other events, 124.4 us)
